TPU v7x, 32 devices: a whole 2x2x4 slice. The times are simulated.
32 devices in a mesh: grp: 2 (over x), aux: 16 (over z, y, core).
Axes of the slice: x: 2, y: 2, z: 4, core: 2. Of those that a mesh axis runs over, the one named last changes fastest.
Arguments:
- three_index: bfloat16 [64, 256, 256], P('aux'), may hold values from -0.375 to 0.375
- relaxed: bfloat16 [512, 256], P('grp'), parts along dimension 0, may hold values from -0.375 to 0.375
- plus_amplitude: bfloat16 [512, 256], P('grp'), parts along dimension 0, may hold values from -0.375 to 0.375
- minus_amplitude: bfloat16 [512, 256], P('grp'), parts along dimension 0, may hold values from -0.375 to 0.375
- ground: bfloat16 [256, 256], replicated, may hold values from -0.375 to 0.375
- integral_grad: bfloat16 [3, 64, 512, 256], P(None, None, 'aux'), may hold values from -0.09375 to 0.09375
- metric_grad: bfloat16 [3, 64, 64], P(None, 'aux'), may hold values from -0.5 to 0.5
- function_atom: int32 [256], replicated, may hold values from 0 to 31, never falling along the last dimension, each value on 1 to 16 neighbouring positions
- aux_center: int32 [64], P('aux'), may hold values from 0 to 31, never falling along the last dimension, each value on 1 to 4 neighbouring positions
- block_list: int32 [512], replicated, may hold values from 0 to 255, as said below
- block_count: int32 [16], replicated, may hold values from 0 to 32, as said below
Outputs:
- gradient: float32 [3, 64], P(None, 'grp'), parts along dimension 1
There are 2 independent parts, one for each index of `grp`. A program takes and returns all parts, laid end to end along the dimension named above; an argument that names none is the same for every part. Nothing has to cross between parts.
Inputs may be any that keep to these rules, and one draw needn't show every extreme that they name: block_count[d] is the number of live slots of owner d; the counts sum to 256, and at least one owner has 32. `block_list`: slot s of owner d is entry d * 32 + s and is live when s < block_count[d]; each tile pair i * 16 + j is held by exactly one live slot; slots that are not live hold arbitrary tile pairs.
All inputs are finite; a program needn't handle non-finite values.
Results may differ from a plain program's by a relative error of at most 0.0032.
Values may be sent and summed in bfloat16 or wider, within the bound.
No kernel may reach another device: no remote copies, remote signals or barrier semaphores. Data moves between devices by JAX's collectives and lax.ppermute only.
A program may use at most 64 MiB of HBM per device.

v0:
```python
import jax
import jax.numpy as jnp
from jax import lax
from jax.sharding import PartitionSpec as P

TILE = 16
NATOM = 32


def on_device(
    three_index,
    relaxed,
    plus_amplitude,
    minus_amplitude,
    ground,
    integral_grad,
    metric_grad,
    function_atom,
    aux_center,
    block_list,
    block_count,
):
    highest = lax.Precision.HIGHEST
    aux_local = three_index.shape[0]
    basis_count = three_index.shape[1]
    tile_count = basis_count // TILE
    slot_depth = integral_grad.shape[2]
    slot_total = block_list.shape[0]
    fitted = jnp.einsum("pab,ab->p", three_index, relaxed, preferred_element_type=jnp.float32)
    stacked = jnp.concatenate([plus_amplitude, minus_amplitude, ground], 0)
    halves = jnp.einsum(
        "ab,pbc->pac", stacked, three_index, preferred_element_type=jnp.float32
    ).astype(jnp.bfloat16)
    paired_half = halves[:, : 2 * basis_count].reshape(aux_local, 2, basis_count, basis_count)
    paired_half = jnp.concatenate([paired_half[:, 0], paired_half[:, 1]], axis=2)
    ground_half = halves[:, 2 * basis_count :]
    partners = jnp.concatenate([plus_amplitude, -minus_amplitude], axis=1)
    exchange_part = jnp.einsum(
        "pab,cb->pac", paired_half, partners, preferred_element_type=jnp.float32
    )
    crossed = jnp.einsum("pab,bc->pac", ground_half, relaxed, preferred_element_type=jnp.float32)
    triple = (
        fitted[:, None, None] * relaxed.astype(jnp.float32)[None]
        + exchange_part
        + crossed
        + jnp.swapaxes(crossed, 1, 2)
    )
    triple = triple.astype(jnp.bfloat16)
    blocked = triple.reshape(aux_local, tile_count, TILE, tile_count, TILE).transpose(0, 1, 3, 2, 4)
    blocked = blocked.reshape(aux_local, tile_count * tile_count, TILE * TILE)
    chosen = jnp.take(blocked, block_list, axis=1)
    slot_ids = jnp.arange(slot_total, dtype=jnp.int32)
    live_mask = (slot_ids % slot_depth < block_count[slot_ids // slot_depth]).astype(jnp.float32)
    arrived = lax.all_to_all(chosen, "aux", split_axis=1, concat_axis=0, tiled=True)
    first_slot = lax.axis_index("aux") * slot_depth
    tile_ids = lax.dynamic_slice_in_dim(block_list, first_slot, slot_depth)
    slot_mask = lax.dynamic_slice_in_dim(live_mask, first_slot, slot_depth)
    contracted = jnp.einsum(
        "pgf,kpgf->kgf", arrived, integral_grad, preferred_element_type=jnp.float32
    )
    slot_count = tile_ids.shape[0]
    row_sums = contracted.reshape(3, slot_count, TILE, TILE).sum(axis=3) * slot_mask[None, :, None]
    function_ids = (tile_ids // tile_count)[:, None] * TILE + jnp.arange(TILE, dtype=jnp.int32)[
        None, :
    ]
    atom_table = (
        function_atom[function_ids][:, :, None] == jnp.arange(NATOM, dtype=jnp.int32)[None, None, :]
    ).astype(jnp.float32)
    three_part = 2.0 * jnp.einsum("kgm,gma->ka", row_sums, atom_table, precision=highest)
    all_fitted = lax.all_gather(fitted, "aux", axis=0, tiled=True)
    coupling = jnp.einsum(
        "kpq,q->kp", metric_grad.astype(jnp.float32), all_fitted, precision=highest
    )
    aux_table = (aux_center[:, None] == jnp.arange(NATOM, dtype=jnp.int32)[None, :]).astype(
        jnp.float32
    )
    metric_part = jnp.einsum("kp,pa->ka", coupling * fitted[None, :], aux_table, precision=highest)
    return lax.psum(three_part - metric_part, "aux")


def solution(mesh):
    in_specs = (
        P("aux", None, None),
        P("grp", None),
        P("grp", None),
        P("grp", None),
        P(),
        P(None, None, "aux", None),
        P(None, "aux", None),
        P(),
        P("aux"),
        P(),
        P(),
    )
    out_specs = P(None, "grp")
    return jax.shard_map(
        on_device, mesh=mesh, in_specs=in_specs, out_specs=out_specs, check_vma=False
    )
```

profile of v0, /device:TPU:0, one launch (start us, length us, event | category | flops | bytes accessed | tf_op | source)
XLA Modules:
  0.0 119.7 jit_solution(17670021363365028496)
XLA Ops:
  0.0 0.0 copy-start
  0.0 1.8 %fusion = bf16[4,768,256]{2,1,0:T(8,128)(2,1)S(1)} fusion(bf16[4,256,256]{2,1,0:T(8,128)(2,1)} %param.11, bf16[256,256]{1,0:T(8,128)(2,1)} %param.15, bf16[256,256]{1,0:T(8,128)(2,1)} %param.14, bf16[256,256]{1,0:T(8,128)(2,1)} %param.13), kind=kOutput, calls=%fused_computation.5 | convolution fusion | flops 404619264 | bytes 2490368 | tf_op jit(solution)/shard_map/ab,pbc->pac/dot_general | solution.py:31
  1.9 0.0 copy-start.6
  1.9 0.0 copy-start.10
  1.9 0.1 slice.37
  2.0 0.0 copy-done.8
  2.0 0.3 fusion.8
  2.3 0.5 copy-done.6
  2.8 0.7 neg.3
  3.4 0.0 copy-done.10
  3.5 0.0 copy-start.4
  3.5 0.9 slice_bitcast_fusion.1
  4.3 0.3 copy.42
  4.7 0.0 copy-start.3
  4.7 0.0 copy-start.7
  4.7 0.0 copy-done.4
  4.7 1.9 %convolution_bitcast_fusion.1 = f32[4]{0:T(128)S(1)} fusion(bf16[4,256,256]{2,1,0:T(8,128)(2,1)S(1)} %copy-done.4, bf16[256,256,1]{1,0,2:T(8,128)(2,1)} %bitcast.80), kind=kOutput, calls=%fused_computation.13 | convolution fusion | flops 524288 | bytes 655376 | tf_op jit(solution)/shard_map/pab,ab->p/dot_general | solution.py:29
  6.6 0.5 copy-done.11
  7.1 0.0 copy-done.5
  7.1 0.0 copy-done.3
  7.1 0.0 copy-done.7
  7.1 0.5 fusion.3
  7.6 4.2 %reshape.108 = bf16[4,16,16,16,16]{4,3,2,1,0:T(8,128)(2,1)} reshape(bf16[4,256,256]{2,1,0:T(8,128)(2,1)S(1)} %fusion.3) | data formatting | bytes 1048576 | tf_op jit(solution)/shard_map/reshape | solution.py:49
  11.7 5.2 %copy.74 = bf16[4,16,16,16,16]{4,2,3,1,0:T(8,128)(2,1)} copy(bf16[4,16,16,16,16]{4,3,2,1,0:T(8,128)(2,1)} %reshape.108) | data formatting | bytes 1048576 | tf_op jit(solution)/shard_map/reshape | solution.py:49
  17.0 5.5 %reshape.109 = bf16[4,256,256]{2,1,0:T(8,128)(2,1)S(1)} reshape(bf16[4,16,16,16,16]{4,3,2,1,0:T(8,128)(2,1)} %bitcast.77) | data formatting | bytes 1048576 | tf_op jit(solution)/shard_map/reshape | solution.py:50
  22.5 0.4 copy.44
  22.9 2.4 %gather_fusion = bf16[512,4,256]{2,1,0:T(4,128)(2,1)S(1)} fusion(bf16[4,256,256]{2,0,1:T(4,128)(2,1)S(1)} %copy.44, s32[1024]{0:T(1024)S(1)} %pad_clamp_fusion.1), kind=kCustom, calls=%fused_computation | custom fusion | bytes 2099200 | tf_op jit(solution)/shard_map/jit(_take)/gather | solution.py:51
  25.3 0.0 copy-start.9
  25.3 0.0 copy-start.1
  25.3 2.7 %select_bitcast_fusion = bf16[4,512,256]{2,0,1:T(4,128)(2,1)} fusion(bf16[512,4,256]{2,1,0:T(4,128)(2,1)S(1)} %gather_fusion, pred[512]{0:T(512)(128)(4,1)S(1)} %compare_and_fusion), kind=kLoop, calls=%fused_computation.18 | loop fusion | flops 524288 | bytes 2097664 | tf_op jit(solution)/shard_map/jit(_take)/select_n | solution.py:51
  28.0 7.4 %all-to-all-start = ((bf16[4,512,256]{2,0,1:T(4,128)(2,1)}), bf16[4,512,256]{2,0,1:T(4,128)(2,1)S(1)}, u32[]{:S(2)}, u32[]{:S(2)}) async-start(bf16[4,512,256]{2,0,1:T(4,128)(2,1)} %select_bitcast_fusion), calls=%async_computation | async-start | bytes 2097152 | tf_op jit(solution)/shard_map/all_to_all | solution.py:54
  35.7 0.0 copy-done.9
  35.7 0.7 fusion.34
  36.5 4.3 %compare_select_fusion.2 = s32[512,1]{0,1:T(1,128)S(1)} fusion(s32[]{:T(128)} %bitcast.30, s32[]{:T(128)} %bitcast.31, s32[]{:T(128)} %bitcast.32, s32[]{:T(128)} %bitcast.33, s32[]{:T(128)} %bitcast.34, s32[]{:T(128)} %bitcast.36, s32[]{:T(128)} %bitcast.35), kind=kLoop, calls=%fused_computation.49 | loop fusion | flops 11776 | bytes 2076 | tf_op jit(solution)/shard_map/gather | solution.py:53
  40.8 5.7 %fusion.25 = f32[512]{0:T(512)S(1)} fusion(pred[512]{0:T(512)(128)(4,1)S(1)} %compare_reduce_fusion, pred[512]{0:T(512)(128)(4,1)S(1)} %compare_reduce_fusion.1, pred[512]{0:T(512)(128)(4,1)S(1)} %compare_reduce_fusion.2, pred[512]{0:T(512)(128)(4,1)S(1)} %compare_reduce_fusion.3, pred[512]{0:T(512)(128)(4,1)S(1)} %compare_reduce_fusion.4, ...), kind=kLoop, calls=%fused_computation.73 | loop fusion | flops 8704 | bytes 8740 | tf_op jit(solution)/shard_map/convert_element_type | solution.py:53
  46.4 0.1 dynamic_slice.6
  46.5 0.1 fusion.28
  46.6 0.1 compare_select_fusion
  46.7 0.1 reshape.144
  46.8 0.0 copy-done.1
  46.8 0.0 copy-start.14
  46.8 0.0 copy-start.12
  46.8 3.5 %gather_fusion.1 = s32[512]{0:T(512)S(1)} fusion(s32[256]{0:T(256)S(1)} %copy-done.1, s32[1024]{0:T(1024)S(1)} %pad_clamp_fusion), kind=kCustom, calls=%fused_computation.1 | custom fusion | bytes 6144 | tf_op jit(solution)/shard_map/gather | solution.py:67
  50.3 0.1 reshape.143
  50.4 0.1 copy.46
  50.5 0.0 copy-done.14
  50.5 0.6 dynamic-slice
  51.7 0.0 copy-done.12
  51.7 0.2 dynamic-update-slice
  52.0 33.9 %all-reduce = f32[64]{0:T(128)S(1)} all-reduce(f32[64]{0:T(128)S(1)} %dynamic-update-slice), channel_id=1, replica_groups=mesh['grp'=2,'aux'=16] {'aux'}, use_global_device_ids=true, to_apply=%add | all-reduce | flops 64 | bytes 512
  85.9 0.0 copy-done
  85.9 0.1 fusion.29
  86.0 0.0 all-to-all-done
  86.1 0.2 copy.59
  86.3 0.0 copy-start.2
  86.3 0.3 bitcast_convert_fusion
  86.6 1.5 %copy-done.2 = bf16[3,64,32,256]{3,2,1,0:T(8,128)(2,1)S(1)} copy-done((bf16[3,64,32,256]{3,2,1,0:T(8,128)(2,1)S(1)}, bf16[3,64,32,256]{3,2,1,0:T(8,128)(2,1)}, u32[]{:S(2)}) %copy-start.2) | copy-done | bytes 3145752
  88.2 0.7 multiply_reduce_fusion
  88.9 0.2 copy.57
  89.1 0.1 bitcast_reduce_fusion
  89.2 0.3 fusion.4
  89.5 0.0 copy-done.13
  89.5 0.2 convolution_subtract_fusion
  89.7 30.1 %psum.7 = f32[3,32]{1,0:T(4,128)} all-reduce(f32[3,32]{1,0:T(4,128)S(1)} %convolution_subtract_fusion), channel_id=1, replica_groups=mesh['grp'=2,'aux'=16] {'aux'}, use_global_device_ids=true, to_apply=%region_1.2 | all-reduce | flops 96 | bytes 768 | tf_op jit(solution)/shard_map/psum | solution.py:78
  (20 shorter events, 0.4 us)
Async XLA Ops:
  0.0 85.9 %copy-start = (bf16[3,4,64]{2,1,0:T(4,128)(2,1)S(1)}, bf16[3,4,64]{2,1,0:T(4,128)(2,1)}, u32[]{:S(2)}) copy-start(bf16[3,4,64]{2,1,0:T(4,128)(2,1)} %param.17) | copy-start | bytes 4612
  0.0 2.0 %copy-start.8 = (bf16[256,256]{1,0:T(8,128)(2,1)S(1)}, bf16[256,256]{1,0:T(8,128)(2,1)}, u32[]{:S(2)}) copy-start(bf16[256,256]{1,0:T(8,128)(2,1)} %param.12) | copy-start | bytes 393220
  1.9 0.9 copy-start.6
  1.9 1.6 %copy-start.10 = (s32[512]{0:T(512)S(1)}, s32[512]{0:T(512)}, u32[]{:S(2)}) copy-start(s32[512]{0:T(512)} %param.20) | copy-start | bytes 6148
  3.5 1.2 %copy-start.4 = (bf16[4,256,256]{2,1,0:T(8,128)(2,1)S(1)}, bf16[4,256,256]{2,1,0:T(8,128)(2,1)}, u32[]{:S(2)}) copy-start(bf16[4,256,256]{2,1,0:T(8,128)(2,1)} %param.11) | copy-start | bytes 1572868
  4.3 2.8 %copy-start.5 = (bf16[256,256]{1,0:T(8,128)(2,1)S(1)}, bf16[256,256]{1,0:T(8,128)(2,1)}, u32[]{:S(2)}) copy-start(bf16[256,256]{1,0:T(8,128)(2,1)} %param.13) | copy-start | bytes 393220
  4.7 2.4 %copy-start.3 = (bf16[4,256,256]{2,1,0:T(8,128)(2,1)S(1)}, bf16[4,256,256]{2,1,0:T(8,128)(2,1)}, u32[]{:S(2)}) copy-start(bf16[4,256,256]{2,1,0:T(8,128)(2,1)} %get-tuple-element.6) | copy-start | bytes 1572868
  4.7 2.4 %copy-start.7 = (bf16[256,256]{1,0:T(8,128)(2,1)S(1)}, bf16[256,256]{1,0:T(8,128)(2,1)}, u32[]{:S(2)}) copy-start(bf16[256,256]{1,0:T(8,128)(2,1)} %neg.3) | copy-start | bytes 393220
  6.6 0.5 copy-start.11
  25.3 10.4 %copy-start.9 = (s32[16]{0:T(128)S(1)}, s32[16]{0:T(128)}, u32[]{:S(2)}) copy-start(s32[16]{0:T(128)} %param.21) | copy-start | bytes 196
  25.3 21.4 %copy-start.1 = (s32[256]{0:T(256)S(1)}, s32[256]{0:T(256)}, u32[]{:S(2)}) copy-start(s32[256]{0:T(256)} %param.18) | copy-start | bytes 3076
  28.0 58.0 %all-to-all-start = ((bf16[4,512,256]{2,0,1:T(4,128)(2,1)}), bf16[4,512,256]{2,0,1:T(4,128)(2,1)S(1)}, u32[]{:S(2)}, u32[]{:S(2)}) async-start(bf16[4,512,256]{2,0,1:T(4,128)(2,1)} %select_bitcast_fusion), calls=%async_computation | async-start | bytes 2097152 | tf_op jit(solution)/shard_map/all_to_all | solution.py:54
  46.8 3.7 %copy-start.14 = (u32[32]{0:T(128)S(1)}, u32[32]{0:T(128)}, u32[]{:S(2)}) copy-start(u32[32]{0:T(128)} %constant.97) | copy-start | bytes 388
  46.8 4.9 %copy-start.12 = (f32[4]{0:T(128)S(1)}, f32[4]{0:T(128)}, u32[]{:S(2)}) copy-start(f32[4]{0:T(128)} %copy-done.11) | copy-start | bytes 52
  86.3 1.9 %copy-start.2 = (bf16[3,64,32,256]{3,2,1,0:T(8,128)(2,1)S(1)}, bf16[3,64,32,256]{3,2,1,0:T(8,128)(2,1)}, u32[]{:S(2)}) copy-start(bf16[3,64,32,256]{3,2,1,0:T(8,128)(2,1)} %param.16) | copy-start | bytes 9437188
  88.2 1.3 %copy-start.13 = (s32[4]{0:T(128)S(1)}, s32[4]{0:T(128)}, u32[]{:S(2)}) copy-start(s32[4]{0:T(128)} %param.19) | copy-start | bytes 52
where the time goes:
time: 120 us
  blocking collectives  64 us (53%)
  local copies, waits for them, and re-layouts  27.3 us (23%)
  other arithmetic  15 us (12%)
  starting transfers between devices  7.41 us (6%)
  matrix products  5.13 us (4%)
    unnamed x1, blocking collectives  33.9 us
    psum x1, blocking collectives, on_device(): return lax.psum(three_part - metric_part, 'aux')  30.1 us
    reshape x2, local copies, waits for them, and re-layouts, on_device(): triple.reshape(aux_local, tile_count, TILE, tile_count, TILE)  9.39 us
    all_to_all x1, starting transfers between devices, on_device(): lax.all_to_all(chosen, 'aux', split_axis=1, concat_axis=0, tiled=True)  7.41 us
    reshape x2, local copies, waits for them, and re-layouts, on_device(): blocked = blocked.reshape(aux_local, tile_count * tile_count, TILE * TILE)  5.89 us
    convert_element_type x1, other arithmetic, on_device(): (slot_ids % slot_depth < block_count[slot_ids // slot_depth]).astype(jnp....  5.67 us
    gather x10, other arithmetic, on_device(): block_count[slot_ids // slot_depth]  4.61 us
    gather x3, local copies, waits for them, and re-layouts, on_device(): function_atom[function_ids][:, :, None]  3.67 us
  transfers between devices with their start and end apart: 1, of which 0 were waited for; matrix products, arithmetic and copies ran while one was open for 13% of the time, Pallas kernels for 0%

commit v1 on v0

--- a/solution.py
+++ b/solution.py
@@ -51,7 +51,10 @@
     chosen = jnp.take(blocked, block_list, axis=1)
     slot_ids = jnp.arange(slot_total, dtype=jnp.int32)
     live_mask = (slot_ids % slot_depth < block_count[slot_ids // slot_depth]).astype(jnp.float32)
-    arrived = lax.all_to_all(chosen, "aux", split_axis=1, concat_axis=0, tiled=True)
+    arrived = jnp.concatenate(
+        lax.all_to_all(jnp.stack(jnp.split(chosen, lax.axis_size("aux"), axis=1)), "aux", 0, 0),
+        axis=0,
+    )
     first_slot = lax.axis_index("aux") * slot_depth
     tile_ids = lax.dynamic_slice_in_dim(block_list, first_slot, slot_depth)
     slot_mask = lax.dynamic_slice_in_dim(live_mask, first_slot, slot_depth)

time: 120 us -> 130 us (1.083)
  local copies, waits for them, and re-layouts: 27.3 us -> 37.6 us
    unnamed x34 -> x49, local copies, waits for them, and re-layouts: 3.64 us -> 13.3 us
  transfers between devices with their start and end apart: 1 -> 1, of which waited for: 0 -> 0; matrix products, arithmetic and copies ran while one was open for 13% -> 12% of each run, Pallas kernels for 0% -> 0%
where the time goes in v1:
time: 130 us; the launch traced here: 129 us
  blocking collectives  64 us (49%)
  local copies, waits for them, and re-layouts  37.6 us (29%)
  other arithmetic  14.1 us (11%)
  starting transfers between devices  7.41 us (6%)
  matrix products  5.13 us (4%)
    unnamed x1, blocking collectives  33.9 us
    psum x1, blocking collectives, on_device(): return lax.psum(three_part - metric_part, 'aux')  30.1 us
    unnamed x49, local copies, waits for them, and re-layouts  13.3 us
    reshape x2, local copies, waits for them, and re-layouts, on_device(): triple.reshape(aux_local, tile_count, TILE, tile_count, TILE)  9.39 us
    all_to_all x1, starting transfers between devices, on_device(): lax.all_to_all(jnp.stack(jnp.split(chosen, lax.axis_size('aux'), axis=1))...  7.41 us
    reshape x2, local copies, waits for them, and re-layouts, on_device(): blocked = blocked.reshape(aux_local, tile_count * tile_count, TILE * TILE)  5.89 us
    convert_element_type x1, other arithmetic, on_device(): (slot_ids % slot_depth < block_count[slot_ids // slot_depth]).astype(jnp....  5.67 us
    gather x10, other arithmetic, on_device(): block_count[slot_ids // slot_depth]  4.61 us
  transfers between devices with their start and end apart: 1, of which 0 were waited for; matrix products, arithmetic and copies ran while one was open for 12% of the time, Pallas kernels for 0%

profile of v1, /device:TPU:0, one launch (start us, length us, event | category | flops | bytes accessed | tf_op | source)
XLA Modules:
  0.0 129.1 jit_solution(2760419318186880401)
XLA Ops:
  0.0 0.0 copy-start
  0.0 1.8 %fusion = bf16[4,768,256]{2,1,0:T(8,128)(2,1)S(1)} fusion(bf16[4,256,256]{2,1,0:T(8,128)(2,1)} %param.11, bf16[256,256]{1,0:T(8,128)(2,1)} %param.15, bf16[256,256]{1,0:T(8,128)(2,1)} %param.14, bf16[256,256]{1,0:T(8,128)(2,1)} %param.13), kind=kOutput, calls=%fused_computation.5 | convolution fusion | flops 404619264 | bytes 2490368 | tf_op jit(solution)/shard_map/ab,pbc->pac/dot_general | solution.py:31
  1.9 0.0 copy-start.6
  1.9 0.0 copy-start.10
  1.9 0.1 slice.37
  2.0 0.3 fusion.8
  2.3 0.5 copy-done.6
  2.8 0.7 neg.3
  3.5 0.1 fusion.44
  3.5 0.1 compare_select_fusion
  3.6 0.1 reshape.148
  3.7 0.9 slice_bitcast_fusion.1
  4.6 0.3 copy.42
  4.9 1.9 %convolution_bitcast_fusion.1 = f32[4]{0:T(128)S(1)} fusion(bf16[4,256,256]{2,1,0:T(8,128)(2,1)S(1)} %copy-done.4, bf16[256,256,1]{1,0,2:T(8,128)(2,1)} %bitcast.140), kind=kOutput, calls=%fused_computation.13 | convolution fusion | flops 524288 | bytes 655376 | tf_op jit(solution)/shard_map/pab,ab->p/dot_general | solution.py:29
  6.8 0.5 copy-done.11
  7.3 0.0 copy-done.5
  7.3 0.5 fusion.3
  7.8 4.2 %reshape.111 = bf16[4,16,16,16,16]{4,3,2,1,0:T(8,128)(2,1)} reshape(bf16[4,256,256]{2,1,0:T(8,128)(2,1)S(1)} %fusion.3) | data formatting | bytes 1048576 | tf_op jit(solution)/shard_map/reshape | solution.py:49
  12.0 5.2 %copy.74 = bf16[4,16,16,16,16]{4,2,3,1,0:T(8,128)(2,1)} copy(bf16[4,16,16,16,16]{4,3,2,1,0:T(8,128)(2,1)} %reshape.111) | data formatting | bytes 1048576 | tf_op jit(solution)/shard_map/reshape | solution.py:49
  17.2 5.5 %reshape.112 = bf16[4,256,256]{2,1,0:T(8,128)(2,1)S(1)} reshape(bf16[4,16,16,16,16]{4,3,2,1,0:T(8,128)(2,1)} %bitcast.138) | data formatting | bytes 1048576 | tf_op jit(solution)/shard_map/reshape | solution.py:50
  22.7 0.4 copy.44
  23.1 2.4 %gather_fusion = bf16[512,4,256]{2,1,0:T(4,128)(2,1)S(1)} fusion(bf16[4,256,256]{2,0,1:T(4,128)(2,1)S(1)} %copy.44, s32[1024]{0:T(1024)S(1)} %get-tuple-element.24), kind=kCustom, calls=%fused_computation | custom fusion | bytes 2099200 | tf_op jit(solution)/shard_map/jit(_take)/gather | solution.py:51
  25.5 1.8 %select_bitcast_fusion = bf16[4,512,256]{2,0,1:T(4,128)(2,1)S(1)} fusion(bf16[512,4,256]{2,1,0:T(4,128)(2,1)S(1)} %gather_fusion, pred[512]{0:T(512)(128)(4,1)S(1)} %compare_and_fusion), kind=kLoop, calls=%fused_computation.18 | loop fusion | flops 524288 | bytes 2097664 | tf_op jit(solution)/shard_map/jit(_take)/select_n | solution.py:51
  27.3 0.0 copy-start.9
  27.4 0.6 fusion.34
  28.0 0.6 fusion.33
  28.6 0.6 fusion.32
  29.3 0.6 fusion.31
  29.9 0.6 fusion.30
  30.6 0.7 fusion.29
  31.2 0.6 fusion.28
  31.9 0.6 fusion.27
  32.5 0.6 fusion.26
  33.1 0.6 fusion.25
  33.8 0.6 fusion.24
  34.4 0.6 fusion.23
  35.1 0.6 fusion.22
  35.7 0.6 fusion.21
  36.3 0.6 fusion.20
  37.0 0.7 fusion.19
  37.6 7.4 %all-to-all-start = ((bf16[16,4,32,256]{3,1,2,0:T(4,128)(2,1)}), bf16[16,4,32,256]{3,1,2,0:T(4,128)(2,1)S(1)}, u32[]{:S(2)}, u32[]{:S(2)}) async-start(bf16[16,4,32,256]{3,1,2,0:T(4,128)(2,1)} %fusion.19), calls=%async_computation | async-start | bytes 2097152 | tf_op jit(solution)/shard_map/all_to_all | solution.py:55
  45.4 0.7 fusion.50
  46.1 4.3 %compare_select_fusion.2 = s32[512,1]{0,1:T(1,128)S(1)} fusion(s32[]{:T(128)} %bitcast.43, s32[]{:T(128)} %bitcast.44, s32[]{:T(128)} %bitcast.45, s32[]{:T(128)} %bitcast.46, s32[]{:T(128)} %bitcast.47, s32[]{:T(128)} %bitcast.49, s32[]{:T(128)} %bitcast.48), kind=kLoop, calls=%fused_computation.81 | loop fusion | flops 11776 | bytes 2076 | tf_op jit(solution)/shard_map/gather | solution.py:53
  50.4 5.7 %fusion.41 = f32[512]{0:T(512)S(1)} fusion(pred[512]{0:T(512)(128)(4,1)S(1)} %compare_reduce_fusion, pred[512]{0:T(512)(128)(4,1)S(1)} %compare_reduce_fusion.1, pred[512]{0:T(512)(128)(4,1)S(1)} %compare_reduce_fusion.2, pred[512]{0:T(512)(128)(4,1)S(1)} %compare_reduce_fusion.3, pred[512]{0:T(512)(128)(4,1)S(1)} %compare_reduce_fusion.4, ...), kind=kLoop, calls=%fused_computation.105 | loop fusion | flops 8704 | bytes 8740 | tf_op jit(solution)/shard_map/convert_element_type | solution.py:53
  56.1 0.1 dynamic_slice.6
  56.2 0.0 copy-done.1
  56.2 3.5 %gather_fusion.1 = s32[512]{0:T(512)S(1)} fusion(s32[256]{0:T(256)S(1)} %copy-done.1, s32[1024]{0:T(1024)S(1)} %get-tuple-element.23), kind=kCustom, calls=%fused_computation.1 | custom fusion | bytes 6144 | tf_op jit(solution)/shard_map/gather | solution.py:70
  59.7 0.1 reshape.147
  59.8 0.1 copy.46
  59.8 0.6 dynamic-slice
  61.1 0.2 dynamic-update-slice
  61.3 33.9 %all-reduce = f32[64]{0:T(128)S(1)} all-reduce(f32[64]{0:T(128)S(1)} %dynamic-update-slice), channel_id=1, replica_groups=mesh['grp'=2,'aux'=16] {'aux'}, use_global_device_ids=true, to_apply=%add | all-reduce | flops 64 | bytes 512
  95.3 0.1 fusion.45
  95.4 0.0 all-to-all-done
  95.4 0.2 copy.59
  95.7 0.0 copy-start.2
  95.7 0.3 bitcast_convert_fusion
  96.0 1.5 %copy-done.2 = bf16[3,64,32,256]{3,2,1,0:T(8,128)(2,1)S(1)} copy-done((bf16[3,64,32,256]{3,2,1,0:T(8,128)(2,1)S(1)}, bf16[3,64,32,256]{3,2,1,0:T(8,128)(2,1)}, u32[]{:S(2)}) %copy-start.2) | copy-done | bytes 3145752
  97.6 0.7 multiply_reduce_fusion
  98.3 0.2 copy.57
  98.5 0.1 bitcast_reduce_fusion
  98.6 0.3 fusion.4
  98.9 0.2 convolution_subtract_fusion
  99.1 30.1 %psum.7 = f32[3,32]{1,0:T(4,128)} all-reduce(f32[3,32]{1,0:T(4,128)S(1)} %convolution_subtract_fusion), channel_id=1, replica_groups=mesh['grp'=2,'aux'=16] {'aux'}, use_global_device_ids=true, to_apply=%region_1.2 | all-reduce | flops 96 | bytes 768 | tf_op jit(solution)/shard_map/psum | solution.py:81
  (35 shorter events, 0.4 us)
Async XLA Ops:
  0.0 95.3 %copy-start = (bf16[3,4,64]{2,1,0:T(4,128)(2,1)S(1)}, bf16[3,4,64]{2,1,0:T(4,128)(2,1)}, u32[]{:S(2)}) copy-start(bf16[3,4,64]{2,1,0:T(4,128)(2,1)} %param.17) | copy-start | bytes 4612
  0.0 2.0 %copy-start.8 = (bf16[256,256]{1,0:T(8,128)(2,1)S(1)}, bf16[256,256]{1,0:T(8,128)(2,1)}, u32[]{:S(2)}) copy-start(bf16[256,256]{1,0:T(8,128)(2,1)} %param.12) | copy-start | bytes 393220
  1.9 0.9 copy-start.6
  1.9 1.6 %copy-start.10 = (s32[512]{0:T(512)S(1)}, s32[512]{0:T(512)}, u32[]{:S(2)}) copy-start(s32[512]{0:T(512)} %param.20) | copy-start | bytes 6148
  3.7 1.2 copy-start.4
  4.6 2.8 %copy-start.5 = (bf16[256,256]{1,0:T(8,128)(2,1)S(1)}, bf16[256,256]{1,0:T(8,128)(2,1)}, u32[]{:S(2)}) copy-start(bf16[256,256]{1,0:T(8,128)(2,1)} %param.13) | copy-start | bytes 393220
  4.9 2.4 %copy-start.3 = (bf16[4,256,256]{2,1,0:T(8,128)(2,1)S(1)}, bf16[4,256,256]{2,1,0:T(8,128)(2,1)}, u32[]{:S(2)}) copy-start(bf16[4,256,256]{2,1,0:T(8,128)(2,1)} %get-tuple-element.6) | copy-start | bytes 1572868
  4.9 2.4 %copy-start.7 = (bf16[256,256]{1,0:T(8,128)(2,1)S(1)}, bf16[256,256]{1,0:T(8,128)(2,1)}, u32[]{:S(2)}) copy-start(bf16[256,256]{1,0:T(8,128)(2,1)} %neg.3) | copy-start | bytes 393220
  6.8 0.5 copy-start.11
  27.3 18.0 %copy-start.9 = (s32[16]{0:T(128)S(1)}, s32[16]{0:T(128)}, u32[]{:S(2)}) copy-start(s32[16]{0:T(128)} %param.21) | copy-start | bytes 196
  28.0 28.2 %copy-start.1 = (s32[256]{0:T(256)S(1)}, s32[256]{0:T(256)}, u32[]{:S(2)}) copy-start(s32[256]{0:T(256)} %param.18) | copy-start | bytes 3076
  37.6 57.8 %all-to-all-start = ((bf16[16,4,32,256]{3,1,2,0:T(4,128)(2,1)}), bf16[16,4,32,256]{3,1,2,0:T(4,128)(2,1)S(1)}, u32[]{:S(2)}, u32[]{:S(2)}) async-start(bf16[16,4,32,256]{3,1,2,0:T(4,128)(2,1)} %fusion.19), calls=%async_computation | async-start | bytes 2097152 | tf_op jit(solution)/shard_map/all_to_all | solution.py:55
  56.2 3.7 %copy-start.14 = (u32[32]{0:T(128)S(1)}, u32[32]{0:T(128)}, u32[]{:S(2)}) copy-start(u32[32]{0:T(128)} %constant.97) | copy-start | bytes 388
  56.2 4.9 %copy-start.12 = (f32[4]{0:T(128)S(1)}, f32[4]{0:T(128)}, u32[]{:S(2)}) copy-start(f32[4]{0:T(128)} %copy-done.11) | copy-start | bytes 52
  95.7 1.9 %copy-start.2 = (bf16[3,64,32,256]{3,2,1,0:T(8,128)(2,1)S(1)}, bf16[3,64,32,256]{3,2,1,0:T(8,128)(2,1)}, u32[]{:S(2)}) copy-start(bf16[3,64,32,256]{3,2,1,0:T(8,128)(2,1)} %param.16) | copy-start | bytes 9437188
  97.5 1.3 %copy-start.13 = (s32[4]{0:T(128)S(1)}, s32[4]{0:T(128)}, u32[]{:S(2)}) copy-start(s32[4]{0:T(128)} %param.19) | copy-start | bytes 52
